TPU v7x, 32 devices: a whole 2x2x4 slice. The times are simulated.
32 devices in a mesh: slab: 8 (over y, x, core), lev: 4 (over z).
Axes of the slice: x: 2, y: 2, z: 4, core: 2. Of those that a mesh axis runs over, the one named last changes fastest.
Arguments:
- ensemble: float32 [80, 16, 18432], P(None, 'lev', 'slab'), may hold values from -6 to 6
- obs_cell: int32 [2, 256], replicated, may hold values from 0 to 294911, as said below
- obs_value: float32 [2, 256], replicated, may hold values from -6 to 6
- obs_var: float32 [2, 256], replicated, may hold values from 0.3 to 3
- obs_frac: float32 [2, 256], replicated, may hold values from 0 to 1
- loc_column: bfloat16 [2, 256, 18432], P(None, 'lev', 'slab'), may hold values from 0 to 1
- loc_level: float32 [2, 256, 16], P(None, None, 'lev'), may hold values from 0.2 to 1
Outputs:
- analysis: float32 [80, 16, 18432], P(None, 'lev', 'slab')
- prior_mean: float32 [2, 256], replicated
Inputs may be any that keep to these rules, and one draw needn't show every extreme that they name: `obs_cell`: in each block, every device's cells (a level band of 4 levels and a slab of 2304 columns) hold at least one observation, and one of them lies in the slab's last column.
All inputs are finite; a program needn't handle non-finite values.
Results may differ from a plain program's by a relative error of at most 0.0055.
Values may be sent and summed in bfloat16 or wider, within the bound.
A program may use at most 64 MiB of HBM per device.

v0:
```python
import jax
import jax.numpy as jnp
from jax import lax
from jax.sharding import PartitionSpec as P


def obs_stats(prior_obs, obs_val, variance):
    members = prior_obs.shape[1]
    obs_mean = jnp.mean(prior_obs, axis=1)
    deviation = prior_obs - obs_mean[:, None]
    spread = jnp.sum(deviation * deviation, axis=1) / (members - 1.0)
    total_var = spread + variance
    shrink = 1.0 / (1.0 + jnp.sqrt(variance / total_var))
    gain_rows = ((obs_val - obs_mean)[:, None] - deviation * shrink[:, None]) / (
        total_var * (members - 1.0)
    )[:, None]
    return (obs_mean, deviation.astype(jnp.bfloat16), gain_rows.astype(jnp.bfloat16))


def cell_values(current, levels, columns):
    members, lev_rows, slab_cols = current.shape
    local_row = levels - lax.axis_index("lev") * lev_rows
    local_col = columns - lax.axis_index("slab") * slab_cols
    inside = (local_row >= 0) & (local_row < lev_rows) & (local_col >= 0) & (local_col < slab_cols)
    row_safe = jnp.clip(local_row, 0, lev_rows - 1)
    col_safe = jnp.clip(local_col, 0, slab_cols - 1)
    flattened = current.reshape(members, lev_rows * slab_cols)
    picked = jnp.take(flattened, row_safe * slab_cols + col_safe, axis=1)
    return jnp.where(inside[None, :], picked, 0.0).T


def column_table(loc_block, columns):
    rows_local, slab_cols = loc_block.shape
    local_col = columns - lax.axis_index("slab") * slab_cols
    inside = (local_col >= 0) & (local_col < slab_cols)
    col_safe = jnp.clip(local_col, 0, slab_cols - 1)
    picked = jnp.take(loc_block, col_safe, axis=1).astype(jnp.float32)
    picked = jnp.where(inside[None, :], picked, 0.0)
    holder = jnp.zeros((rows_local * lax.axis_size("lev"), columns.shape[0]), jnp.float32)
    return lax.dynamic_update_slice(
        holder, picked, (lax.axis_index("lev") * rows_local, jnp.int32(0))
    )


def level_table(lev_block, levels):
    lev_rows = lev_block.shape[1]
    local_row = levels - lax.axis_index("lev") * lev_rows
    inside = (local_row >= 0) & (local_row < lev_rows) & (lax.axis_index("slab") == 0)
    row_safe = jnp.clip(local_row, 0, lev_rows - 1)
    picked = jnp.take(lev_block, row_safe, axis=1)
    return jnp.where(inside[None, :], picked, 0.0)


def cell_update(values, dev_b, gain_b, col_table, lev_table):
    centred_cells = (values - jnp.mean(values, axis=1)[:, None]).astype(jnp.bfloat16)
    cross_cov = jnp.dot(dev_b, centred_cells.T, preferred_element_type=jnp.float32)
    mixed_rows = (lev_table * col_table * cross_cov).astype(jnp.bfloat16)
    return values + jnp.dot(gain_b.T, mixed_rows, preferred_element_type=jnp.float32).T


def regress_rows(running, loc_piece, centred, dev_b, gain_b, lev_weights):
    row_total = loc_piece.shape[0]
    row_step = min(row_total, 64)
    lev_rows = lev_weights.shape[1]
    slab_cols = loc_piece.shape[1]
    for offset in range(0, row_total, row_step):
        row_count = min(row_step, row_total - offset)
        row_piece = loc_piece[offset : offset + row_count]
        dev_rows = lax.dynamic_slice_in_dim(dev_b, offset, row_count, 0)
        gain_rows = lax.dynamic_slice_in_dim(gain_b, offset, row_count, 0)
        level_loc = lax.dynamic_slice_in_dim(lev_weights, offset, row_count, 0)
        cross_cov = jnp.dot(dev_rows, centred, preferred_element_type=jnp.float32).reshape(
            row_count, lev_rows, slab_cols
        )
        weights = level_loc[:, :, None] * row_piece[:, None, :].astype(jnp.float32)
        mixed_rows = (
            (weights * cross_cov).astype(jnp.bfloat16).reshape(row_count, lev_rows * slab_cols)
        )
        running = running + jnp.dot(gain_rows.T, mixed_rows, preferred_element_type=jnp.float32)
    return running


def on_device(ensemble, obs_cell, obs_value, obs_var, obs_frac, loc_column, loc_level):
    members, lev_rows, slab_cols = ensemble.shape
    n_blocks = obs_cell.shape[0]
    total_cols = slab_cols * lax.axis_size("slab")
    pair_index = {}
    pieces = []
    for later in range(n_blocks):
        levels = obs_cell[later] // total_cols
        columns = obs_cell[later] % total_cols
        next_cols = (columns + 1) % total_cols
        pieces.append(cell_values(ensemble, levels, columns))
        pieces.append(cell_values(ensemble, levels, next_cols))
        for earlier in range(later):
            pair_index[earlier, later] = len(pieces)
            pieces.append(column_table(loc_column[earlier], columns))
            pieces.append(column_table(loc_column[earlier], next_cols))
            pieces.append(level_table(loc_level[earlier], levels))
    summed = lax.psum(tuple(pieces), ("slab", "lev"))
    raw_first = []
    raw_second = []
    position = 0
    for later in range(n_blocks):
        raw_first.append(summed[position])
        raw_second.append(summed[position + 1])
        position = position + 2 + 3 * later
    current = ensemble
    prior_means = []
    for block_index in range(n_blocks):
        fraction = obs_frac[block_index]
        prior_obs = (1.0 - fraction)[:, None] * raw_first[block_index] + fraction[
            :, None
        ] * raw_second[block_index]
        obs_mean, dev_b, gain_b = obs_stats(prior_obs, obs_value[block_index], obs_var[block_index])
        prior_means.append(obs_mean)
        centred = (
            (current - jnp.mean(current, axis=0))
            .astype(jnp.bfloat16)
            .reshape(members, lev_rows * slab_cols)
        )
        lev_weights = loc_level[block_index]
        zero_incr = jnp.zeros((members, lev_rows * slab_cols), jnp.float32)
        increment = regress_rows(
            zero_incr,
            lax.all_gather(loc_column[block_index], "lev", axis=0, tiled=True),
            centred,
            dev_b,
            gain_b,
            lev_weights,
        )
        for later in range(block_index + 1, n_blocks):
            start_at = pair_index[block_index, later]
            col_first = summed[start_at]
            col_second = summed[start_at + 1]
            lev_table = summed[start_at + 2]
            raw_first[later] = cell_update(raw_first[later], dev_b, gain_b, col_first, lev_table)
            raw_second[later] = cell_update(raw_second[later], dev_b, gain_b, col_second, lev_table)
        current = current + increment.reshape(members, lev_rows, slab_cols)
    return (current, jnp.stack(prior_means))


def solution(mesh):
    in_specs = (
        P(None, "lev", "slab"),
        P(),
        P(),
        P(),
        P(),
        P(None, "lev", "slab"),
        P(None, None, "lev"),
    )
    out_specs = (P(None, "lev", "slab"), P())
    return jax.shard_map(
        on_device, mesh=mesh, in_specs=in_specs, out_specs=out_specs, check_vma=False
    )
```

profile of v0, /device:TPU:0, one launch (start us, length us, event | category | flops | bytes accessed | tf_op | source)
XLA Modules:
  0.0 248.2 jit_solution(5838560874919320193)
XLA Ops:
  8.0 0.7 compare_select_fusion
  8.8 0.7 compare_and_fusion.1
  9.5 0.8 fusion.80
  10.2 0.8 and_reduce_fusion.6
  11.2 5.2 %copy.43 = f32[80,4,2304]{0,2,1:T(8,128)} copy(f32[80,4,2304]{2,1,0:T(4,128)} %param.11) | data formatting | bytes 5898240 | tf_op args[0]
  16.3 3.1 %gather_fusion.3 = f32[256,80]{1,0:T(8,128)S(1)} fusion(f32[80,9216]{0,1:T(8,128)} %bitcast.227, s32[1024]{0:T(1024)S(1)} %pad_clamp_fusion.4), kind=kCustom, calls=%fused_computation.3.clone | custom fusion | bytes 164864 | tf_op jit(solution)/shard_map/jit(_take)/gather | solution.py:28
  19.5 3.1 %gather_fusion.5 = f32[256,80]{1,0:T(8,128)S(1)} fusion(f32[80,9216]{0,1:T(8,128)} %bitcast.228, s32[1024]{0:T(1024)S(1)} %pad_clamp_fusion.1), kind=kCustom, calls=%fused_computation.4.clone | custom fusion | bytes 164864 | tf_op jit(solution)/shard_map/jit(_take)/gather | solution.py:28
  22.6 0.7 fusion.91
  23.3 0.4 copy.70
  23.7 0.9 gather_fusion.4
  24.7 1.0 gather_fusion
  25.7 0.1 copy.54
  25.8 0.9 gather_fusion.6
  26.8 3.1 %gather_fusion.2 = f32[256,80]{1,0:T(8,128)S(1)} fusion(f32[80,9216]{0,1:T(8,128)} %bitcast.229, s32[1024]{0:T(1024)S(1)} %pad_clamp_fusion.5), kind=kCustom, calls=%fused_computation.2.clone | custom fusion | bytes 164864 | tf_op jit(solution)/shard_map/jit(_take)/gather | solution.py:28
  29.8 3.1 %gather_fusion.1 = f32[256,80]{1,0:T(8,128)S(1)} fusion(f32[80,9216]{0,1:T(8,128)} %bitcast.230, s32[1024]{0:T(1024)S(1)} %pad_clamp_fusion.6), kind=kCustom, calls=%fused_computation.clone | custom fusion | bytes 164864 | tf_op jit(solution)/shard_map/jit(_take)/gather | solution.py:28
  32.9 0.8 fusion.52
  33.7 0.8 fusion.51
  34.5 0.7 select_bitcast_fusion
  35.2 0.8 fusion.53
  36.0 0.8 fusion.54
  36.9 0.6 copy-done.7
  37.7 0.5 all-gather.5.cloned.1.call-update
  38.3 0.5 all-gather.7.cloned.1.call-update
  38.9 0.8 fusion.94
  39.7 0.8 fusion.92
  40.4 0.8 fusion.93
  41.2 0.5 reduce_sum.74
  41.7 1.6 subtract_convert_fusion.1
  43.3 154.2 %all-reduce.3.cloned.1.call-done = (f32[256,80]{1,0:T(8,128)}, f32[256,80]{1,0:T(8,128)}, f32[256,80]{1,0:T(8,128)}, f32[256,256]{1,0:T(8,128)}, f32[256,256]{1,...) async-done(((f32[256,80]{1,0:T(8,128)}, f32[256,80]{1,0:T(8,128)}, f32[256,80]{1,0:T(8,128)}, f32[256,256]{1,0:T(8,128)}, f32[256,256]{1,0:T(8,128)}, ...) | async-done | bytes 1114128 | tf_op jit(solution)/shard_map/psum | solution.py:100
  197.6 1.0 reduce_sum.75
  198.6 1.0 reduce_sum.76
  199.7 1.2 fusion.88
  200.9 0.2 multiply_reduce_fusion.1
  201.1 0.2 divide_convert_fusion.1
  201.3 2.3 fusion.32
  203.6 1.7 fusion.95
  205.3 0.2 multiply_reduce_fusion
  205.5 0.6 pad_maximum_fusion
  206.1 0.2 divide_convert_fusion
  206.4 1.5 fusion.45
  207.9 0.2 copy-done.1
  208.1 0.6 fusion.14
  208.7 0.6 fusion.15
  209.4 0.6 fusion.67
  210.0 0.6 fusion.13
  210.6 0.6 fusion.12
  211.3 0.6 convolution_add_fusion.5
  211.8 0.6 convolution_add_fusion.4
  212.4 2.2 convolution_add_fusion.3
  214.6 4.5 %reshape.310 = f32[80,4,2304]{2,1,0:T(4,128)} reshape(f32[80,9216]{1,0:T(8,128)} %convolution_add_fusion.3) | data formatting | bytes 5898240 | tf_op jit(solution)/shard_map/reshape | solution.py:139
  219.1 2.8 %fusion.87 = (f32[4,2304]{1,0:T(4,128)S(1)}, f32[80,4,2304]{2,1,0:T(4,128)S(1)}) fusion(f32[80,4,2304]{2,1,0:T(4,128)S(1)} %copy-done, f32[80,4,2304]{2,1,0:T(4,128)} %reshape.310), kind=kLoop, calls=%fused_computation.218 | loop fusion | flops 1465344 | bytes 8884224 | tf_op jit(solution)/shard_map/reduce_sum | solution.py:118
  221.9 1.6 copy-done.2
  223.4 0.5 subtract_convert_fusion
  224.0 1.4 fusion.41
  225.4 0.6 fusion.8
  226.1 0.6 fusion.9
  226.7 0.6 fusion.10
  227.4 0.6 fusion.11
  228.0 0.6 fusion.62
  228.6 0.6 convolution_add_fusion.2
  229.2 0.6 convolution_add_fusion.1
  229.8 2.2 convolution_add_fusion
  231.9 4.6 %reshape.316 = f32[80,4,2304]{2,1,0:T(4,128)} reshape(f32[80,9216]{1,0:T(8,128)} %convolution_add_fusion) | data formatting | bytes 5898240 | tf_op jit(solution)/shard_map/reshape | solution.py:139
  236.6 4.2 %add.227 = f32[80,4,2304]{2,1,0:T(4,128)} add(f32[80,4,2304]{2,1,0:T(4,128)S(1)} %copy-done.3, f32[80,4,2304]{2,1,0:T(4,128)} %reshape.316) | non-fusion elementwise | flops 737280 | bytes 8847360 | tf_op jit(solution)/shard_map/add | solution.py:139
  (61 shorter events, 1.5 us)
Async XLA Ops:
  8.0 189.6 %all-reduce.3.cloned.1.call-start = ((), (), s32[]{:S(2)}) async-start(), calls=%async_computation.2 | async-start | bytes 2621440 | tf_op jit(solution)/shard_map/psum | solution.py:100
  16.3 6.2 %copy-start.8 = (bf16[2,64,2304]{2,1,0:T(8,128)(2,1)S(1)}, bf16[2,64,2304]{2,1,0:T(8,128)(2,1)}, u32[]{:S(2)}) copy-start(bf16[2,64,2304]{2,1,0:T(8,128)(2,1)} %param.16) | copy-start | bytes 1769476
  19.5 5.2 %copy-start.9 = (f32[2,256,4]{1,2,0:T(4,128)S(1)}, f32[2,256,4]{1,2,0:T(4,128)}, u32[]{:S(2)}) copy-start(f32[2,256,4]{1,2,0:T(4,128)} %param.17) | copy-start | bytes 24580
  23.3 2.3 copy-start.4
  36.0 5.2 %copy-start = (f32[80,4,2304]{2,1,0:T(4,128)S(1)}, f32[80,4,2304]{2,1,0:T(4,128)}, u32[]{:S(2)}) copy-start(f32[80,4,2304]{2,1,0:T(4,128)} %param.11) | copy-start | bytes 8847364
  36.8 0.7 copy-start.7
  36.9 0.7 copy-start.6
  37.7 168.7 %all-gather.5.cloned.1.call-start = ((), (), s32[]{:S(2)}) async-start(), calls=%async_computation | async-start | bytes 1474560 | tf_op jit(solution)/shard_map/all_gather | solution.py:126
  38.2 185.7 %all-gather.7.cloned.1.call-start = ((), (), s32[]{:S(2)}) async-start(), calls=%async_computation.1 | async-start | bytes 1474560 | tf_op jit(solution)/shard_map/all_gather | solution.py:126
  197.6 6.0 %copy-start.5 = (f32[256,256]{1,0:T(8,128)S(1)}, f32[256,256]{1,0:T(8,128)}, u32[]{:S(2)}) copy-start(f32[256,256]{1,0:T(8,128)} %get-tuple-element.16) | copy-start | bytes 786436
  206.4 1.7 copy-start.1
  221.8 1.6 copy-start.2
  231.9 4.7 %copy-start.3 = (f32[80,4,2304]{2,1,0:T(4,128)S(1)}, f32[80,4,2304]{2,1,0:T(4,128)}, u32[]{:S(2)}) copy-start(f32[80,4,2304]{2,1,0:T(4,128)} %copy-done.2) | copy-start | bytes 8847364
Sparse Core Ops, SparseCore 0:
  37.8 159.7 all-reduce.2
Sparse Core Ops, SparseCore 1:
  39.7 35.3 all-gather.4
  76.5 30.3 all-gather.6
where the time goes:
time: 249 us; the launch traced here: 248 us
  waiting for transfers between devices  155 us (62%)
  local copies, waits for them, and re-layouts  36.3 us (15%)
  other arithmetic  24.3 us (10%)
  matrix products  16.2 us (7%)
  between operations  16 us (6%)
    psum x1, waiting for transfers between devices, on_device(): summed = lax.psum(tuple(pieces), ('slab', 'lev'))  154 us
    gather x4, local copies, waits for them, and re-layouts, cell_values(): picked = jnp.take(flattened, row_safe * slab_cols + col_safe, axis=1)  12.3 us
    reshape x2, local copies, waits for them, and re-layouts, on_device(): current = current + increment.reshape(members, lev_rows, slab_cols)  9.14 us
    unnamed x22, local copies, waits for them, and re-layouts  8.05 us
    dot_general x8, matrix products, regress_rows(): jnp.dot(gain_rows.T, mixed_rows, preferred_element_type=jnp.float32)  7.72 us
  transfers between devices with their start and end apart: 3, of which 1 were waited for; matrix products, arithmetic and copies ran while one was open for 12% of the time, Pallas kernels for 0%

commit v1 on v0

v1 whole, which is shorter than its diff:
```python
import functools

import jax
import jax.numpy as jnp
from jax import lax
from jax.experimental import pallas as pl
from jax.experimental.pallas import tpu as pltpu
from jax.sharding import PartitionSpec as P

MESH = pl.DeviceIdType.MESH
LANES = 128
F32 = jnp.float32
BF16 = jnp.bfloat16


def pick_kernel(block, members, lev_rows, n_slab, cell_ref, frac_ref, ens_ref, out_ref, acc):
    n_obs = cell_ref.shape[1]
    tiles = ens_ref.shape[0] // (members * lev_rows)
    slab_cols = tiles * LANES
    total = slab_cols * n_slab
    base = lax.axis_index("lev") * (lev_rows * total)
    col_base = lax.axis_index("slab") * slab_cols
    acc[...] = jnp.zeros_like(acc)
    lane_ids = lax.broadcasted_iota(jnp.int32, (members, LANES), 1)

    def body(j, carry):
        rest = cell_ref[block, j] - base
        frac = frac_ref[block, j]
        row = jnp.int32(0)
        for level in range(1, lev_rows):
            row = row + (rest >= level * total).astype(jnp.int32)
        in_band = (rest >= 0) & (rest < lev_rows * total)
        col = rest - row * total
        following = jnp.where(col + 1 == total, 0, col + 1)
        tile_at = lax.shift_right_logical(j, 7)
        lane_at = j & (LANES - 1)

        def add(column, weight):
            local = column - col_base

            @pl.when(in_band & (local >= 0) & (local < slab_cols))
            def _():
                start = lax.shift_right_logical(local, 7) * lev_rows + row
                window = ens_ref[pl.ds(start, members, stride=tiles * lev_rows), :]
                moved = pltpu.roll(window, (lane_at - (local & (LANES - 1))) & (LANES - 1), 1)
                old = acc[tile_at, :members, :]
                acc[tile_at, :members, :] = old + jnp.where(lane_ids == lane_at, moved * weight, 0.0)

        add(col, 1.0 - frac)
        add(following, frac)
        return carry

    lax.fori_loop(0, n_obs, body, 0)
    for t in range(n_obs // LANES):
        out_ref[t * LANES : (t + 1) * LANES, :] = acc[t].T


def pick(block, n_slab, members, lev_rows, cells, fracs, flat):
    n_obs = cells.shape[1]
    return pl.pallas_call(
        functools.partial(pick_kernel, block, members, lev_rows, n_slab),
        out_shape=jax.ShapeDtypeStruct((n_obs, LANES), F32),
        in_specs=[
            pl.BlockSpec(memory_space=pltpu.SMEM),
            pl.BlockSpec(memory_space=pltpu.SMEM),
            pl.BlockSpec(memory_space=pltpu.VMEM),
        ],
        out_specs=pl.BlockSpec(memory_space=pltpu.VMEM),
        scratch_shapes=[pltpu.VMEM((n_obs // LANES, LANES, LANES), F32)],
        name="pick",
    )(cells, fracs, flat)


def exchange_kernel(
    n_slab, n_lev, pieces, part_ref, loc_ref, prior_ref, gat_ref, landed, own,
    scat_send, scat_recv, cast_send, cast_recv, up_send, down_send, line_recv,
):
    n = n_slab * n_lev
    slab, lev = lax.axis_index("slab"), lax.axis_index("lev")
    me = slab * n_lev + lev
    rows = loc_ref.shape[1]
    cut = rows // pieces

    def peer(k):
        p = lax.rem(me + k, n)
        return p, (p // n_lev, lax.rem(p, n_lev))

    barrier = pltpu.get_barrier_semaphore()

    def greet(k, c):
        _, where = peer(k)
        pl.semaphore_signal(barrier, inc=1, device_id=where, device_id_type=MESH)
        return c

    lax.fori_loop(1, n, greet, 0)
    pl.semaphore_wait(barrier, n - 1)

    def scatter(k):
        p, where = peer(k)
        return pltpu.make_async_remote_copy(
            src_ref=part_ref.at[p], dst_ref=landed.at[k], send_sem=scat_send.at[k],
            recv_sem=scat_recv.at[k], device_id=where, device_id_type=MESH)

    def cast(k):
        _, where = peer(k)
        return pltpu.make_async_remote_copy(
            src_ref=own, dst_ref=prior_ref.at[me], send_sem=cast_send.at[k],
            recv_sem=cast_recv.at[k], device_id=where, device_id_type=MESH)

    def each(act):
        def body(k, c):
            act(k)
            return c
        lax.fori_loop(1, n, body, 0)

    def slot(source, h):
        return gat_ref.at[pl.ds(pl.multiple_of(source * rows + h * cut, cut), cut), :]

    def hop(source, h, first, step):
        src = loc_ref.at[0, pl.ds(h * cut, cut), :] if first else slot(source, h)
        sems = up_send if step > 0 else down_send
        return pltpu.make_async_remote_copy(
            src_ref=src, dst_ref=slot(source, h), send_sem=sems.at[source, h],
            recv_sem=line_recv.at[source, h], device_id=(slab, lev + step), device_id_type=MESH)

    each(lambda k: scatter(k).start())
    for h in range(pieces):
        @pl.when(lev < n_lev - 1)
        def _():
            hop(lev, h, True, 1).start()

        @pl.when(lev > 0)
        def _():
            hop(lev, h, True, -1).start()

    gat_ref[pl.ds(pl.multiple_of(lev * rows, rows), rows), :] = loc_ref[0]

    each(lambda k: scatter(k).wait_recv())
    landed[0] = part_ref[me]
    own[...] = jnp.sum(landed[...], axis=0)
    each(lambda k: cast(k).start())
    prior_ref[me] = own[...]

    for s in range(1, n_lev):
        for h in range(pieces):
            @pl.when(lev - s >= 0)
            def _():
                hop(lev - s, h, False, 1).wait_recv()

                @pl.when(lev < n_lev - 1)
                def _():
                    hop(lev - s, h, False, 1).start()

            @pl.when(lev + s <= n_lev - 1)
            def _():
                hop(lev + s, h, False, -1).wait_recv()

                @pl.when(lev > 0)
                def _():
                    hop(lev + s, h, False, -1).start()

    each(lambda k: cast(k).wait_recv())
    each(lambda k: scatter(k).wait_send())
    each(lambda k: cast(k).wait_send())
    for s in range(n_lev):
        for h in range(pieces):
            @pl.when((lev - s >= 0) & (lev < n_lev - 1))
            def _():
                hop(lev - s, h, s == 0, 1).wait_send()

            @pl.when((lev + s <= n_lev - 1) & (lev > 0))
            def _():
                hop(lev + s, h, s == 0, -1).wait_send()


def exchange(block, n_slab, n_lev, part, loc):
    n = n_slab * n_lev
    n_obs = part.shape[0]
    per = n_obs // n
    rows, cols = loc.shape[1:]
    pieces = 2
    prior, gathered = pl.pallas_call(
        functools.partial(exchange_kernel, n_slab, n_lev, pieces),
        grid=(1,),
        out_shape=[
            jax.ShapeDtypeStruct((n, per, LANES), F32),
            jax.ShapeDtypeStruct((n_obs, cols), BF16),
        ],
        in_specs=[
            pl.BlockSpec((n, per, LANES), lambda i: (0, 0, 0)),
            pl.BlockSpec((1, rows, cols), lambda i: (block, 0, 0)),
        ],
        out_specs=[
            pl.BlockSpec((n, per, LANES), lambda i: (0, 0, 0)),
            pl.BlockSpec((n_obs, cols), lambda i: (0, 0)),
        ],
        scratch_shapes=[
            pltpu.VMEM((n, per, LANES), F32),
            pltpu.VMEM((per, LANES), F32),
            pltpu.SemaphoreType.DMA((n,)),
            pltpu.SemaphoreType.DMA((n,)),
            pltpu.SemaphoreType.DMA((n,)),
            pltpu.SemaphoreType.DMA((n,)),
            pltpu.SemaphoreType.DMA((n_lev, pieces)),
            pltpu.SemaphoreType.DMA((n_lev, pieces)),
            pltpu.SemaphoreType.DMA((n_lev, pieces)),
        ],
        compiler_params=pltpu.CompilerParams(collective_id=block, has_side_effects=True),
        name="exchange",
    )(part.reshape(n, per, LANES), loc)
    return prior.reshape(n_obs, LANES), gathered


def update_kernel(block, lev_rows, prior_ref, value_ref, var_ref, lev_ref, loc_ref, ens_ref, out_ref, mean_ref, dev_s, gain_s):
    members = ens_ref.shape[0]
    group = ens_ref.shape[1]
    n_obs = prior_ref.shape[0]

    @pl.when(pl.program_id(0) == 0)
    def _():
        def column(ref):
            return jnp.broadcast_to(ref[block : block + 1, :], (8, n_obs)).T[:, :1]

        value, var = column(value_ref), column(var_ref)
        prior = prior_ref[...]
        live = lax.broadcasted_iota(jnp.int32, prior.shape, 1) < members
        mean = jnp.sum(jnp.where(live, prior, 0.0), axis=1, keepdims=True) / members
        deviation = jnp.where(live, prior - mean, 0.0)
        spread = jnp.sum(deviation * deviation, axis=1, keepdims=True) / (members - 1.0)
        total = spread + var
        shrink = 1.0 / (1.0 + jnp.sqrt(var / total))
        gain = ((value - mean) - deviation * shrink) / (total * (members - 1.0))
        dev_s[...] = deviation.astype(BF16)
        gain_s[...] = gain.T.astype(BF16)
        mean_ref[...] = jnp.broadcast_to(mean, (n_obs, LANES)).T[:8, :]

    dev = dev_s[:, :members]
    gain = gain_s[:members, :]
    rows_in = ens_ref.reshape(members * group, LANES)
    rows_out = out_ref.reshape(members * group, LANES)
    tiles = group // lev_rows
    loc = loc_ref[...].astype(F32)
    for level in range(lev_rows):
        spots = [pl.ds(t * lev_rows + level, members, stride=group) for t in range(tiles)]
        now = jnp.concatenate([rows_in[spot, :] for spot in spots], axis=1)
        centred = (now - jnp.sum(now, axis=0, keepdims=True) / members).astype(BF16)
        cross = jnp.dot(dev, centred, preferred_element_type=F32)
        mixed = ((lev_ref[:, level : level + 1] * loc) * cross).astype(BF16)
        new = now + jnp.dot(gain, mixed, preferred_element_type=F32)
        for t, spot in enumerate(spots):
            rows_out[spot, :] = new[:, t * LANES : (t + 1) * LANES]


def update(block, lev_rows, prior, values, variances, levels, gathered, state):
    members, depth, _ = state.shape
    n_obs = prior.shape[0]
    tiles = 2
    group = tiles * lev_rows
    steps = depth // group
    return pl.pallas_call(
        functools.partial(update_kernel, block, lev_rows),
        grid=(steps,),
        out_shape=[
            jax.ShapeDtypeStruct(state.shape, F32),
            jax.ShapeDtypeStruct((8, n_obs), F32),
        ],
        in_specs=[
            pl.BlockSpec((n_obs, LANES), lambda i: (0, 0)),
            pl.BlockSpec(values.shape, lambda i: (0, 0)),
            pl.BlockSpec(values.shape, lambda i: (0, 0)),
            pl.BlockSpec((None, n_obs, lev_rows), lambda i: (block, 0, 0)),
            pl.BlockSpec((n_obs, tiles * LANES), lambda i: (0, i)),
            pl.BlockSpec((members, group, LANES), lambda i: (0, i, 0)),
        ],
        out_specs=[
            pl.BlockSpec((members, group, LANES), lambda i: (0, i, 0)),
            pl.BlockSpec((8, n_obs), lambda i: (0, 0)),
        ],
        scratch_shapes=[pltpu.VMEM((n_obs, LANES), BF16), pltpu.VMEM((LANES, n_obs), BF16)],
        compiler_params=pltpu.CompilerParams(dimension_semantics=("arbitrary",)),
        name="update",
    )(prior, values, variances, levels, gathered, state)


def solution(mesh):
    n_slab, n_lev = mesh.shape["slab"], mesh.shape["lev"]

    def on_device(ensemble, obs_cell, obs_value, obs_var, obs_frac, loc_column, loc_level):
        members, lev_rows, cols = ensemble.shape
        tiles = cols // LANES
        state = ensemble.reshape(members, lev_rows, tiles, LANES).transpose(0, 2, 1, 3)
        state = state.reshape(members, tiles * lev_rows, LANES)
        means = []
        for block in range(obs_cell.shape[0]):
            flat = state.reshape(members * tiles * lev_rows, LANES)
            part = pick(block, n_slab, members, lev_rows, obs_cell, obs_frac, flat)
            prior, gathered = exchange(block, n_slab, n_lev, part, loc_column)
            state, mean = update(block, lev_rows, prior, obs_value, obs_var, loc_level, gathered, state)
            means.append(mean[0])
        analysis = state.reshape(members, tiles, lev_rows, LANES).transpose(0, 2, 1, 3)
        return analysis.reshape(members, lev_rows, cols), jnp.stack(means)

    in_specs = (
        P(None, "lev", "slab"), P(), P(), P(), P(),
        P(None, "lev", "slab"), P(None, None, "lev"),
    )
    return jax.shard_map(
        on_device, mesh=mesh, in_specs=in_specs,
        out_specs=(P(None, "lev", "slab"), P()), check_vma=False,
    )
```

time: 249 us -> 145 us (0.58)
  waiting for transfers between devices: 155 us -> 0 us
  Pallas kernels: 0 us -> 119 us
  other arithmetic: 24.3 us -> 0.59 us
  matrix products: 16.2 us -> 0 us
  between operations: 16 us -> 0.66 us
  local copies, waits for them, and re-layouts: 36.3 us -> 23.6 us
    psum x1 -> x0, waiting for transfers between devices: 154 us -> none  [on_device(): summed = lax.psum(tuple(pieces), ('slab', 'lev'))]
    pallas_call x0 -> x6, Pallas kernels: none -> 119 us  [the longest x2 65.1 us: exchange(): pl.pallas_call(functools.partial(exchange_kernel, n_slab, n_lev, pieces),...]
    dot_general x18 -> x0, matrix products: 16.2 us -> none  [the longest x8 7.72 us: regress_rows(): jnp.dot(gain_rows.T, mixed_rows, preferred_element_type=jnp.float32)]
    gather x10 -> x0, local copies, waits for them, and re-layouts: 15.3 us -> none  [the longest x4 12.3 us: cell_values(): picked = jnp.take(flattened, row_safe * slab_cols + col_safe, axis=1)]
    reduce_sum x7 -> x0, other arithmetic: 6.89 us -> none  [the longest x2 3.28 us: on_device(): jnp.mean(current, axis=0)]
    transpose x0 -> x1, local copies, waits for them, and re-layouts: none -> 5.61 us  [on_device(): ensemble.reshape(members, lev_rows, tiles, LANES).transpose(0, 2, 1, 3)]
    convert_element_type x6 -> x0, other arithmetic: 5.51 us -> none  [the longest x2 2.95 us: regress_rows(): weights = level_loc[:, :, None] * row_piece[:, None, :].astype(jnp.float32)]
    add x1 -> x0, other arithmetic: 4.19 us -> none  [on_device(): current = current + increment.reshape(members, lev_rows, slab_cols)]
  transfers between devices with their start and end apart: 3 -> 0, of which waited for: 1 -> 0; matrix products, arithmetic and copies ran while one was open for 12% -> 0% of each run, Pallas kernels for 0% -> 0%
where the time goes in v1:
time: 145 us; the launch traced here: 144 us
  Pallas kernels  119 us (82%)
  local copies, waits for them, and re-layouts  23.6 us (16%)
    pallas_call x2, Pallas kernels, exchange(): pl.pallas_call(functools.partial(exchange_kernel, n_slab, n_lev, pieces),...  65.1 us
    pallas_call x2, Pallas kernels, pick(): pl.pallas_call(functools.partial(pick_kernel, block, members, lev_rows, n...  29.8 us
    pallas_call x2, Pallas kernels, update(): pl.pallas_call(functools.partial(update_kernel, block, lev_rows), grid=(s...  24.2 us
    unnamed x3, local copies, waits for them, and re-layouts  7.43 us
    transpose x1, local copies, waits for them, and re-layouts, on_device(): ensemble.reshape(members, lev_rows, tiles, LANES).transpose(0, 2, 1, 3)  5.61 us
    reshape x1, local copies, waits for them, and re-layouts, on_device(): state.reshape(members, tiles, lev_rows, LANES).transpose(0, 2, 1, 3)  4.03 us
    reshape x1, local copies, waits for them, and re-layouts, on_device(): return (analysis.reshape(members, lev_rows, cols), jnp.stack(means))  3.05 us

profile of v1, /device:TPU:0, one launch (start us, length us, event | category | flops | bytes accessed | tf_op | source)
XLA Modules:
  0.0 144.0 jit_solution(18159872090951486775)
XLA Ops:
  0.6 1.5 %copy.16.lev_ref = f32[2,256,4]{2,1,0:T(8,128)} copy(f32[2,256,4]{1,2,0:T(4,128)} %param.13) | data formatting | bytes 16384 | tf_op args[6]
  2.2 2.4 %copy.13 = f32[80,4,2304]{2,0,1:T(8,128)S(1)} copy(f32[80,4,2304]{2,1,0:T(4,128)} %param.7) | data formatting | bytes 5898240 | tf_op args[0]
  4.6 2.1 %reshape.31 = f32[80,4,18,128]{3,2,0,1:T(8,128)} reshape(f32[80,4,2304]{2,0,1:T(8,128)S(1)} %copy.13) | data formatting | bytes 5898240 | tf_op jit(solution)/shard_map/reshape | solution.py:291
  6.7 5.6 %copy.14 = f32[80,18,4,128]{3,2,1,0:T(4,128)} copy(f32[80,18,4,128]{3,1,0,2:T(8,128)} %bitcast.18) | data formatting | bytes 5898240 | tf_op jit(solution)/shard_map/transpose | solution.py:291
  12.3 15.3 %pick.2 = f32[256,128]{1,0:T(8,128)} custom-call(s32[2,256]{1,0:T(2,128)} %cell_ref.3, f32[2,256]{1,0:T(2,128)} %frac_ref.3, f32[5760,128]{1,0:T(8,128)} %bitcast.16), custom_call_target="tpu_custom_call" | custom-call | tf_op jit(solution)/shard_map/pick/pallas_call | solution.py:60
  27.6 33.8 %exchange.2 = (f32[32,8,128]{2,1,0:T(8,128)}, bf16[256,2304]{1,0:T(8,128)(2,1)}) custom-call(f32[32,8,128]{2,1,0:T(8,128)} %bitcast.22, bf16[2,64,2304]{2,1,0:T(8,128)(2,1)} %loc_ref.3), custom_call_target="tpu_custom_call" | custom-call | tf_op jit(solution)/shard_map/exchange/pallas_call | solution.py:182
  61.4 12.1 %update.2 = (f32[80,72,128]{2,1,0:T(8,128)}, f32[8,256]{1,0:T(8,128)}) custom-call(f32[256,128]{1,0:T(8,128)} %bitcast.25, f32[2,256]{1,0:T(2,128)} %value_ref.3, f32[2,256]{1,0:T(2,128)} %var_ref.3, f32[2,256,4]{2,1,0:T(8,128)} %copy.16.lev_ref, bf16[256,2304]{1,0:T(8,128)(2,1)} %get-tuple-element.11.loc_ref, f32[80,72,128]{2,1,0:T(8,128)} %bitcast.17), custom_call_target="tpu_custom_call" | custom-call | tf_op jit(solution)/shard_map/update/pallas_call | solution.py:260
  73.5 0.7 slice.6
  74.2 14.4 %pick.3 = f32[256,128]{1,0:T(8,128)} custom-call(s32[2,256]{1,0:T(2,128)} %cell_ref.3, f32[2,256]{1,0:T(2,128)} %frac_ref.3, f32[5760,128]{1,0:T(8,128)} %bitcast.20), custom_call_target="tpu_custom_call" | custom-call | tf_op jit(solution)/shard_map/pick/pallas_call | solution.py:60
  88.7 31.4 %exchange.3 = (f32[32,8,128]{2,1,0:T(8,128)}, bf16[256,2304]{1,0:T(8,128)(2,1)}) custom-call(f32[32,8,128]{2,1,0:T(8,128)} %bitcast.23, bf16[2,64,2304]{2,1,0:T(8,128)(2,1)} %loc_ref.3), custom_call_target="tpu_custom_call" | custom-call | tf_op jit(solution)/shard_map/exchange/pallas_call | solution.py:182
  120.0 12.1 %update.3 = (f32[80,72,128]{2,1,0:T(8,128)}, f32[8,256]{1,0:T(8,128)}) custom-call(f32[256,128]{1,0:T(8,128)} %bitcast.24, f32[2,256]{1,0:T(2,128)} %value_ref.3, f32[2,256]{1,0:T(2,128)} %var_ref.3, f32[2,256,4]{2,1,0:T(8,128)} %copy.16.lev_ref, bf16[256,2304]{1,0:T(8,128)(2,1)} %get-tuple-element.14.loc_ref, f32[80,72,128]{2,1,0:T(8,128)} %get-tuple-element.12.ens_ref), custom_call_target="tpu_custom_call" | custom-call | tf_op jit(solution)/shard_map/update/pallas_call | solution.py:260
  132.1 0.7 slice.7
  132.8 0.6 pad_maximum_fusion
  133.4 4.0 %copy.21 = f32[80,18,4,128]{3,1,0,2:T(8,128)} copy(f32[80,18,4,128]{3,2,1,0:T(4,128)} %bitcast.21) | data formatting | bytes 5898240 | tf_op jit(solution)/shard_map/reshape | solution.py:300
  137.4 3.1 %reshape.39 = f32[80,4,2304]{2,0,1:T(8,128)S(1)} reshape(f32[80,4,18,128]{3,2,0,1:T(8,128)} %bitcast.19) | data formatting | bytes 5898240 | tf_op jit(solution)/shard_map/reshape | solution.py:301
  140.5 3.5 %copy.19 = f32[80,4,2304]{2,1,0:T(4,128)} copy(f32[80,4,2304]{2,0,1:T(8,128)S(1)} %reshape.39) | data formatting | bytes 5898240

commit v2 on v1

--- a/solution.py
+++ b/solution.py
@@ -13,9 +13,10 @@
 BF16 = jnp.bfloat16
 
 
-def pick_kernel(block, members, lev_rows, n_slab, cell_ref, frac_ref, ens_ref, out_ref, acc):
+def pick_kernel(block, members, lev_rows, n_slab, cell_ref, frac_ref, ens_ref, out_ref, acc, list_ref):
     n_obs = cell_ref.shape[1]
-    tiles = ens_ref.shape[0] // (members * lev_rows)
+    raw = len(ens_ref.shape) == 3
+    tiles = ens_ref.shape[2] // LANES if raw else ens_ref.shape[0] // (members * lev_rows)
     slab_cols = tiles * LANES
     total = slab_cols * n_slab
     base = lax.axis_index("lev") * (lev_rows * total)
@@ -23,34 +24,52 @@
     acc[...] = jnp.zeros_like(acc)
     lane_ids = lax.broadcasted_iota(jnp.int32, (members, LANES), 1)
 
-    def body(j, carry):
+    def place(j):
         rest = cell_ref[block, j] - base
-        frac = frac_ref[block, j]
         row = jnp.int32(0)
         for level in range(1, lev_rows):
             row = row + (rest >= level * total).astype(jnp.int32)
-        in_band = (rest >= 0) & (rest < lev_rows * total)
         col = rest - row * total
         following = jnp.where(col + 1 == total, 0, col + 1)
+        first, second = col - col_base, following - col_base
+        in_band = (rest >= 0) & (rest < lev_rows * total)
+        has_first = in_band & (first >= 0) & (first < slab_cols)
+        has_second = in_band & (second >= 0) & (second < slab_cols)
+        return row, first, second, has_first, has_second
+
+    def scan(j, count):
+        _, _, _, has_first, has_second = place(j)
+        list_ref[count] = j
+        return count + (has_first | has_second).astype(jnp.int32)
+
+    count = lax.fori_loop(0, n_obs, scan, jnp.int32(0), unroll=8)
+
+    def body(at, carry):
+        j = list_ref[at]
+        row, first, second, has_first, has_second = place(j)
+        frac = frac_ref[block, j]
         tile_at = lax.shift_right_logical(j, 7)
         lane_at = j & (LANES - 1)
 
-        def add(column, weight):
-            local = column - col_base
-
-            @pl.when(in_band & (local >= 0) & (local < slab_cols))
-            def _():
-                start = lax.shift_right_logical(local, 7) * lev_rows + row
-                window = ens_ref[pl.ds(start, members, stride=tiles * lev_rows), :]
-                moved = pltpu.roll(window, (lane_at - (local & (LANES - 1))) & (LANES - 1), 1)
-                old = acc[tile_at, :members, :]
-                acc[tile_at, :members, :] = old + jnp.where(lane_ids == lane_at, moved * weight, 0.0)
-
-        add(col, 1.0 - frac)
-        add(following, frac)
+        def share(local, weight, mine):
+            local = jnp.where(mine, local, 0)
+            tile = lax.shift_right_logical(local, 7)
+            if raw:
+                lanes = pl.ds(pl.multiple_of(tile * LANES, LANES), LANES)
+                window = ens_ref[:, 0, lanes]
+                for level in range(1, lev_rows):
+                    window = jnp.where(row == level, ens_ref[:, level, lanes], window)
+            else:
+                window = ens_ref[pl.ds(tile * lev_rows + row, members, stride=tiles * lev_rows), :]
+            moved = pltpu.roll(window, (lane_at - (local & (LANES - 1))) & (LANES - 1), 1)
+            return moved * jnp.where(mine, weight, 0.0)
+
+        value = share(first, 1.0 - frac, has_first) + share(second, frac, has_second)
+        old = acc[tile_at, :members, :]
+        acc[tile_at, :members, :] = jnp.where(lane_ids == lane_at, value, old)
         return carry
 
-    lax.fori_loop(0, n_obs, body, 0)
+    lax.fori_loop(0, count, body, 0)
     for t in range(n_obs // LANES):
         out_ref[t * LANES : (t + 1) * LANES, :] = acc[t].T
 
@@ -66,7 +85,7 @@
             pl.BlockSpec(memory_space=pltpu.VMEM),
         ],
         out_specs=pl.BlockSpec(memory_space=pltpu.VMEM),
-        scratch_shapes=[pltpu.VMEM((n_obs // LANES, LANES, LANES), F32)],
+        scratch_shapes=[pltpu.VMEM((n_obs // LANES, LANES, LANES), F32), pltpu.SMEM((n_obs + 1,), jnp.int32)],
         name="pick",
     )(cells, fracs, flat)
 
@@ -211,10 +230,11 @@
     return prior.reshape(n_obs, LANES), gathered
 
 
-def update_kernel(block, lev_rows, prior_ref, value_ref, var_ref, lev_ref, loc_ref, ens_ref, out_ref, mean_ref, dev_s, gain_s):
+def update_kernel(block, lev_rows, raw_in, raw_out, prior_ref, value_ref, var_ref, lev_ref, old_ref, loc_ref, ens_ref, out_ref, mean_ref, dev_s, gain_s, lev_s):
     members = ens_ref.shape[0]
-    group = ens_ref.shape[1]
     n_obs = prior_ref.shape[0]
+    tiles = loc_ref.shape[1] // LANES
+    group = tiles * lev_rows
 
     @pl.when(pl.program_id(0) == 0)
     def _():
@@ -232,54 +252,69 @@
         gain = ((value - mean) - deviation * shrink) / (total * (members - 1.0))
         dev_s[...] = deviation.astype(BF16)
         gain_s[...] = gain.T.astype(BF16)
-        mean_ref[...] = jnp.broadcast_to(mean, (n_obs, LANES)).T[:8, :]
+        mean_ref[...] = old_ref[...]
+        mean_ref[block : block + 1, :] = jnp.broadcast_to(mean, (n_obs, LANES)).T[:1, :]
+        for level in range(lev_rows):
+            lev_s[level] = jnp.broadcast_to(lev_ref[level : level + 1, :], (LANES, n_obs)).T
 
     dev = dev_s[:, :members]
     gain = gain_s[:members, :]
-    rows_in = ens_ref.reshape(members * group, LANES)
-    rows_out = out_ref.reshape(members * group, LANES)
-    tiles = group // lev_rows
+    rows_in = None if raw_in else ens_ref.reshape(members * group, LANES)
+    rows_out = None if raw_out else out_ref.reshape(members * group, LANES)
     loc = loc_ref[...].astype(F32)
     for level in range(lev_rows):
         spots = [pl.ds(t * lev_rows + level, members, stride=group) for t in range(tiles)]
-        now = jnp.concatenate([rows_in[spot, :] for spot in spots], axis=1)
+        if raw_in:
+            now = ens_ref[:, level, :]
+        else:
+            now = jnp.concatenate([rows_in[spot, :] for spot in spots], axis=1)
         centred = (now - jnp.sum(now, axis=0, keepdims=True) / members).astype(BF16)
         cross = jnp.dot(dev, centred, preferred_element_type=F32)
-        mixed = ((lev_ref[:, level : level + 1] * loc) * cross).astype(BF16)
+        height = jnp.concatenate([lev_s[level]] * tiles, axis=1)
+        mixed = ((height * loc) * cross).astype(BF16)
         new = now + jnp.dot(gain, mixed, preferred_element_type=F32)
-        for t, spot in enumerate(spots):
-            rows_out[spot, :] = new[:, t * LANES : (t + 1) * LANES]
-
-
-def update(block, lev_rows, prior, values, variances, levels, gathered, state):
-    members, depth, _ = state.shape
+        if raw_out:
+            out_ref[:, level, :] = new
+        else:
+            for t, spot in enumerate(spots):
+                rows_out[spot, :] = new[:, t * LANES : (t + 1) * LANES]
+
+
+def update(block, n_blocks, lev_rows, prior, values, variances, levels, olds, gathered, state):
+    members = state.shape[0]
     n_obs = prior.shape[0]
-    tiles = 2
+    tiles = next(t for t in (6, 4, 2) if gathered.shape[1] % (t * LANES) == 0)
     group = tiles * lev_rows
-    steps = depth // group
+    cols = gathered.shape[1]
+    steps = cols // (tiles * LANES)
+    raw_in, raw_out = block == 0, block == n_blocks - 1
+    raw_spec = pl.BlockSpec((members, lev_rows, tiles * LANES), lambda i: (0, 0, i))
+    row_spec = pl.BlockSpec((members, group, LANES), lambda i: (0, i, 0))
+    out_dims = (members, lev_rows, cols) if raw_out else (members, steps * group, LANES)
     return pl.pallas_call(
-        functools.partial(update_kernel, block, lev_rows),
+        functools.partial(update_kernel, block, lev_rows, raw_in, raw_out),
         grid=(steps,),
         out_shape=[
-            jax.ShapeDtypeStruct(state.shape, F32),
-            jax.ShapeDtypeStruct((8, n_obs), F32),
+            jax.ShapeDtypeStruct(out_dims, F32),
+            jax.ShapeDtypeStruct(values.shape, F32),
         ],
         in_specs=[
             pl.BlockSpec((n_obs, LANES), lambda i: (0, 0)),
             pl.BlockSpec(values.shape, lambda i: (0, 0)),
             pl.BlockSpec(values.shape, lambda i: (0, 0)),
-            pl.BlockSpec((None, n_obs, lev_rows), lambda i: (block, 0, 0)),
+            pl.BlockSpec((None, lev_rows, n_obs), lambda i: (block, 0, 0)),
+            pl.BlockSpec(olds.shape, lambda i: (0, 0)),
             pl.BlockSpec((n_obs, tiles * LANES), lambda i: (0, i)),
-            pl.BlockSpec((members, group, LANES), lambda i: (0, i, 0)),
+            raw_spec if raw_in else row_spec,
         ],
         out_specs=[
-            pl.BlockSpec((members, group, LANES), lambda i: (0, i, 0)),
-            pl.BlockSpec((8, n_obs), lambda i: (0, 0)),
-        ],
-        scratch_shapes=[pltpu.VMEM((n_obs, LANES), BF16), pltpu.VMEM((LANES, n_obs), BF16)],
+            raw_spec if raw_out else row_spec,
+            pl.BlockSpec(values.shape, lambda i: (0, 0)),
+        ],
+        scratch_shapes=[pltpu.VMEM((n_obs, LANES), BF16), pltpu.VMEM((LANES, n_obs), BF16), pltpu.VMEM((lev_rows, n_obs, LANES), F32)],
         compiler_params=pltpu.CompilerParams(dimension_semantics=("arbitrary",)),
         name="update",
-    )(prior, values, variances, levels, gathered, state)
+    )(prior, values, variances, levels, olds, gathered, state)
 
 
 def solution(mesh):
@@ -287,18 +322,15 @@
 
     def on_device(ensemble, obs_cell, obs_value, obs_var, obs_frac, loc_column, loc_level):
         members, lev_rows, cols = ensemble.shape
-        tiles = cols // LANES
-        state = ensemble.reshape(members, lev_rows, tiles, LANES).transpose(0, 2, 1, 3)
-        state = state.reshape(members, tiles * lev_rows, LANES)
-        means = []
-        for block in range(obs_cell.shape[0]):
-            flat = state.reshape(members * tiles * lev_rows, LANES)
+        n_blocks = obs_cell.shape[0]
+        state = ensemble
+        means, heights = obs_value, loc_level.transpose(0, 2, 1)
+        for block in range(n_blocks):
+            flat = state if block == 0 else state.reshape(members * cols // LANES * lev_rows, LANES)
             part = pick(block, n_slab, members, lev_rows, obs_cell, obs_frac, flat)
             prior, gathered = exchange(block, n_slab, n_lev, part, loc_column)
-            state, mean = update(block, lev_rows, prior, obs_value, obs_var, loc_level, gathered, state)
-            means.append(mean[0])
-        analysis = state.reshape(members, tiles, lev_rows, LANES).transpose(0, 2, 1, 3)
-        return analysis.reshape(members, lev_rows, cols), jnp.stack(means)
+            state, means = update(block, n_blocks, lev_rows, prior, obs_value, obs_var, heights, means, gathered, state)
+        return state, means
 
     in_specs = (
         P(None, "lev", "slab"), P(), P(), P(), P(),

time: 145 us -> 103 us (0.71)
  local copies, waits for them, and re-layouts: 23.6 us -> 0 us
  Pallas kernels: 119 us -> 102 us
    pallas_call x2, Pallas kernels: 29.8 us -> 20.6 us  [pick(): pl.pallas_call(functools.partial(pick_kernel, block, members, lev_rows, n...]
    reshape x3 -> x0, local copies, waits for them, and re-layouts: 9.17 us -> none  [the longest x1 4.03 us: on_device(): state.reshape(members, tiles, lev_rows, LANES).transpose(0, 2, 1, 3)]
    pallas_call x2, Pallas kernels: 24.2 us -> 15.4 us  [update(): pl.pallas_call(functools.partial(update_kernel, block, lev_rows, raw_in,...]
    unnamed x3 -> x0, local copies, waits for them, and re-layouts: 7.43 us -> none
    transpose x1 -> x0, local copies, waits for them, and re-layouts: 5.61 us -> none  [on_device(): ensemble.reshape(members, lev_rows, tiles, LANES).transpose(0, 2, 1, 3)]
where the time goes in v2:
time: 103 us; the launch traced here: 102 us
  Pallas kernels  102 us (99%)
    pallas_call x2, Pallas kernels, exchange(): pl.pallas_call(functools.partial(exchange_kernel, n_slab, n_lev, pieces),...  65.9 us
    pallas_call x2, Pallas kernels, pick(): pl.pallas_call(functools.partial(pick_kernel, block, members, lev_rows, n...  20.6 us
    pallas_call x2, Pallas kernels, update(): pl.pallas_call(functools.partial(update_kernel, block, lev_rows, raw_in,...  15.4 us

profile of v2, /device:TPU:0, one launch (start us, length us, event | category | flops | bytes accessed | tf_op | source)
XLA Modules:
  0.0 102.5 jit_solution(17693455362925994347)
XLA Ops:
  0.6 11.6 %pick.2 = f32[256,128]{1,0:T(8,128)} custom-call(s32[2,256]{1,0:T(2,128)} %cell_ref.3, f32[2,256]{1,0:T(2,128)} %frac_ref.3, f32[80,4,2304]{2,1,0:T(4,128)} %ens_ref.3), custom_call_target="tpu_custom_call" | custom-call | tf_op jit(solution)/shard_map/pick/pallas_call | solution.py:79
  12.2 35.4 %exchange.2 = (f32[32,8,128]{2,1,0:T(8,128)}, bf16[256,2304]{1,0:T(8,128)(2,1)}) custom-call(f32[32,8,128]{2,1,0:T(8,128)} %bitcast.7, bf16[2,64,2304]{2,1,0:T(8,128)(2,1)} %loc_ref.3), custom_call_target="tpu_custom_call" | custom-call | tf_op jit(solution)/shard_map/exchange/pallas_call | solution.py:201
  47.6 8.0 %update.2 = (f32[80,72,128]{2,1,0:T(8,128)}, f32[2,256]{1,0:T(2,128)}) custom-call(f32[256,128]{1,0:T(8,128)} %bitcast.10, f32[2,256]{1,0:T(2,128)} %value_ref.3, f32[2,256]{1,0:T(2,128)} %var_ref.3, f32[2,4,256]{2,1,0:T(4,128)} %bitcast.11, f32[2,256]{1,0:T(2,128)} %value_ref.3, bf16[256,2304]{1,0:T(8,128)(2,1)} %get-tuple-element.9.loc_ref, ...), custom_call_target="tpu_custom_call" | custom-call | tf_op jit(solution)/shard_map/update/pallas_call | solution.py:294
  55.6 9.0 %pick.3 = f32[256,128]{1,0:T(8,128)} custom-call(s32[2,256]{1,0:T(2,128)} %cell_ref.3, f32[2,256]{1,0:T(2,128)} %frac_ref.3, f32[5760,128]{1,0:T(8,128)} %bitcast.6), custom_call_target="tpu_custom_call" | custom-call | tf_op jit(solution)/shard_map/pick/pallas_call | solution.py:79
  64.6 30.5 %exchange.3 = (f32[32,8,128]{2,1,0:T(8,128)}, bf16[256,2304]{1,0:T(8,128)(2,1)}) custom-call(f32[32,8,128]{2,1,0:T(8,128)} %bitcast.8, bf16[2,64,2304]{2,1,0:T(8,128)(2,1)} %loc_ref.3), custom_call_target="tpu_custom_call" | custom-call | tf_op jit(solution)/shard_map/exchange/pallas_call | solution.py:201
  95.1 7.4 %update.3 = (f32[80,4,2304]{2,1,0:T(4,128)}, f32[2,256]{1,0:T(2,128)}) custom-call(f32[256,128]{1,0:T(8,128)} %bitcast.9, f32[2,256]{1,0:T(2,128)} %value_ref.3, f32[2,256]{1,0:T(2,128)} %var_ref.3, f32[2,4,256]{2,1,0:T(4,128)} %bitcast.12, f32[2,256]{1,0:T(2,128)} %get-tuple-element.12.old_ref, bf16[256,2304]{1,0:T(8,128)(2,1)} %get-tuple-element.13.loc_ref, ...), custom_call_target="tpu_custom_call" | custom-call | tf_op jit(solution)/shard_map/update/pallas_call | solution.py:294

commit v3 on v2

--- a/solution.py
+++ b/solution.py
@@ -51,22 +51,26 @@
         tile_at = lax.shift_right_logical(j, 7)
         lane_at = j & (LANES - 1)
 
-        def share(local, weight, mine):
+        def share(local, weight, mine, level):
             local = jnp.where(mine, local, 0)
             tile = lax.shift_right_logical(local, 7)
             if raw:
-                lanes = pl.ds(pl.multiple_of(tile * LANES, LANES), LANES)
-                window = ens_ref[:, 0, lanes]
-                for level in range(1, lev_rows):
-                    window = jnp.where(row == level, ens_ref[:, level, lanes], window)
+                window = ens_ref[:, level, pl.ds(pl.multiple_of(tile * LANES, LANES), LANES)]
             else:
                 window = ens_ref[pl.ds(tile * lev_rows + row, members, stride=tiles * lev_rows), :]
             moved = pltpu.roll(window, (lane_at - (local & (LANES - 1))) & (LANES - 1), 1)
             return moved * jnp.where(mine, weight, 0.0)
 
-        value = share(first, 1.0 - frac, has_first) + share(second, frac, has_second)
-        old = acc[tile_at, :members, :]
-        acc[tile_at, :members, :] = jnp.where(lane_ids == lane_at, value, old)
+        def put(level):
+            value = share(first, 1.0 - frac, has_first, level) + share(second, frac, has_second, level)
+            old = acc[tile_at, :members, :]
+            acc[tile_at, :members, :] = jnp.where(lane_ids == lane_at, value, old)
+
+        if raw:
+            for level in range(lev_rows):
+                pl.when(row == level)(functools.partial(put, level))
+        else:
+            put(0)
         return carry
 
     lax.fori_loop(0, count, body, 0)
@@ -135,22 +139,27 @@
     def slot(source, h):
         return gat_ref.at[pl.ds(pl.multiple_of(source * rows + h * cut, cut), cut), :]
 
+    def up_hops(h):
+        return n_lev // 2 - (n_lev % 2 == 0 and h >= pieces // 2)
+
+    def hops(h, step):
+        return up_hops(h) if step > 0 else n_lev - 1 - up_hops(h)
+
+    def back(s):
+        return lax.rem(lev + s + n_lev, n_lev)
+
     def hop(source, h, first, step):
         src = loc_ref.at[0, pl.ds(h * cut, cut), :] if first else slot(source, h)
         sems = up_send if step > 0 else down_send
         return pltpu.make_async_remote_copy(
             src_ref=src, dst_ref=slot(source, h), send_sem=sems.at[source, h],
-            recv_sem=line_recv.at[source, h], device_id=(slab, lev + step), device_id_type=MESH)
+            recv_sem=line_recv.at[source, h], device_id=(slab, back(step)), device_id_type=MESH)
 
     each(lambda k: scatter(k).start())
     for h in range(pieces):
-        @pl.when(lev < n_lev - 1)
-        def _():
-            hop(lev, h, True, 1).start()
-
-        @pl.when(lev > 0)
-        def _():
-            hop(lev, h, True, -1).start()
+        for step in (1, -1):
+            if hops(h, step) > 0:
+                hop(lev, h, True, step).start()
 
     gat_ref[pl.ds(pl.multiple_of(lev * rows, rows), rows), :] = loc_ref[0]
 
@@ -160,36 +169,19 @@
     each(lambda k: cast(k).start())
     prior_ref[me] = own[...]
 
-    for s in range(1, n_lev):
-        for h in range(pieces):
-            @pl.when(lev - s >= 0)
-            def _():
-                hop(lev - s, h, False, 1).wait_recv()
-
-                @pl.when(lev < n_lev - 1)
-                def _():
-                    hop(lev - s, h, False, 1).start()
-
-            @pl.when(lev + s <= n_lev - 1)
-            def _():
-                hop(lev + s, h, False, -1).wait_recv()
-
-                @pl.when(lev > 0)
-                def _():
-                    hop(lev + s, h, False, -1).start()
+    route = [(s, h, step) for s in range(n_lev) for h in range(pieces) for step in (1, -1)]
+    for s, h, step in route:
+        if 1 <= s <= hops(h, step):
+            hop(back(-s * step), h, False, step).wait_recv()
+            if s < hops(h, step):
+                hop(back(-s * step), h, False, step).start()
 
     each(lambda k: cast(k).wait_recv())
     each(lambda k: scatter(k).wait_send())
     each(lambda k: cast(k).wait_send())
-    for s in range(n_lev):
-        for h in range(pieces):
-            @pl.when((lev - s >= 0) & (lev < n_lev - 1))
-            def _():
-                hop(lev - s, h, s == 0, 1).wait_send()
-
-            @pl.when((lev + s <= n_lev - 1) & (lev > 0))
-            def _():
-                hop(lev + s, h, s == 0, -1).wait_send()
+    for s, h, step in route:
+        if s < hops(h, step):
+            hop(back(-s * step), h, s == 0, step).wait_send()
 
 
 def exchange(block, n_slab, n_lev, part, loc):

time: 103 us -> 103 us (level)
  no operation moved by 1% of the time
where the time goes in v3:
time: 103 us; the launch traced here: 102 us
  Pallas kernels  101 us (98%)
    pallas_call x2, Pallas kernels, exchange(): pl.pallas_call(functools.partial(exchange_kernel, n_slab, n_lev, pieces),...  64.9 us
    pallas_call x2, Pallas kernels, pick(): pl.pallas_call(functools.partial(pick_kernel, block, members, lev_rows, n...  21.2 us
    pallas_call x2, Pallas kernels, update(): pl.pallas_call(functools.partial(update_kernel, block, lev_rows, raw_in,...  15.4 us

profile of v3, /device:TPU:0, one launch (start us, length us, event | category | flops | bytes accessed | tf_op | source)
XLA Modules:
  0.0 102.1 jit_solution(575665779239941037)
XLA Ops:
  0.6 11.7 %pick.2 = f32[256,128]{1,0:T(8,128)} custom-call(s32[2,256]{1,0:T(2,128)} %cell_ref.3, f32[2,256]{1,0:T(2,128)} %frac_ref.3, f32[80,4,2304]{2,1,0:T(4,128)} %ens_ref.3), custom_call_target="tpu_custom_call" | custom-call | tf_op jit(solution)/shard_map/pick/pallas_call | solution.py:83
  12.3 32.7 %exchange.2 = (f32[32,8,128]{2,1,0:T(8,128)}, bf16[256,2304]{1,0:T(8,128)(2,1)}) custom-call(f32[32,8,128]{2,1,0:T(8,128)} %bitcast.7, bf16[2,64,2304]{2,1,0:T(8,128)(2,1)} %loc_ref.3), custom_call_target="tpu_custom_call" | custom-call | tf_op jit(solution)/shard_map/exchange/pallas_call | solution.py:193
  45.0 8.0 %update.2 = (f32[80,72,128]{2,1,0:T(8,128)}, f32[2,256]{1,0:T(2,128)}) custom-call(f32[256,128]{1,0:T(8,128)} %bitcast.10, f32[2,256]{1,0:T(2,128)} %value_ref.3, f32[2,256]{1,0:T(2,128)} %var_ref.3, f32[2,4,256]{2,1,0:T(4,128)} %bitcast.11, f32[2,256]{1,0:T(2,128)} %value_ref.3, bf16[256,2304]{1,0:T(8,128)(2,1)} %get-tuple-element.9.loc_ref, ...), custom_call_target="tpu_custom_call" | custom-call | tf_op jit(solution)/shard_map/update/pallas_call | solution.py:286
  53.0 9.6 %pick.3 = f32[256,128]{1,0:T(8,128)} custom-call(s32[2,256]{1,0:T(2,128)} %cell_ref.3, f32[2,256]{1,0:T(2,128)} %frac_ref.3, f32[5760,128]{1,0:T(8,128)} %bitcast.6), custom_call_target="tpu_custom_call" | custom-call | tf_op jit(solution)/shard_map/pick/pallas_call | solution.py:83
  62.5 32.2 %exchange.3 = (f32[32,8,128]{2,1,0:T(8,128)}, bf16[256,2304]{1,0:T(8,128)(2,1)}) custom-call(f32[32,8,128]{2,1,0:T(8,128)} %bitcast.8, bf16[2,64,2304]{2,1,0:T(8,128)(2,1)} %loc_ref.3), custom_call_target="tpu_custom_call" | custom-call | tf_op jit(solution)/shard_map/exchange/pallas_call | solution.py:193
  94.7 7.4 %update.3 = (f32[80,4,2304]{2,1,0:T(4,128)}, f32[2,256]{1,0:T(2,128)}) custom-call(f32[256,128]{1,0:T(8,128)} %bitcast.9, f32[2,256]{1,0:T(2,128)} %value_ref.3, f32[2,256]{1,0:T(2,128)} %var_ref.3, f32[2,4,256]{2,1,0:T(4,128)} %bitcast.12, f32[2,256]{1,0:T(2,128)} %get-tuple-element.12.old_ref, bf16[256,2304]{1,0:T(8,128)(2,1)} %get-tuple-element.13.loc_ref, ...), custom_call_target="tpu_custom_call" | custom-call | tf_op jit(solution)/shard_map/update/pallas_call | solution.py:286

commit v4 on v2

--- a/solution.py
+++ b/solution.py
@@ -51,22 +51,26 @@
         tile_at = lax.shift_right_logical(j, 7)
         lane_at = j & (LANES - 1)
 
-        def share(local, weight, mine):
+        def share(local, weight, mine, level):
             local = jnp.where(mine, local, 0)
             tile = lax.shift_right_logical(local, 7)
             if raw:
-                lanes = pl.ds(pl.multiple_of(tile * LANES, LANES), LANES)
-                window = ens_ref[:, 0, lanes]
-                for level in range(1, lev_rows):
-                    window = jnp.where(row == level, ens_ref[:, level, lanes], window)
+                window = ens_ref[:, level, pl.ds(pl.multiple_of(tile * LANES, LANES), LANES)]
             else:
                 window = ens_ref[pl.ds(tile * lev_rows + row, members, stride=tiles * lev_rows), :]
             moved = pltpu.roll(window, (lane_at - (local & (LANES - 1))) & (LANES - 1), 1)
             return moved * jnp.where(mine, weight, 0.0)
 
-        value = share(first, 1.0 - frac, has_first) + share(second, frac, has_second)
-        old = acc[tile_at, :members, :]
-        acc[tile_at, :members, :] = jnp.where(lane_ids == lane_at, value, old)
+        def put(level):
+            value = share(first, 1.0 - frac, has_first, level) + share(second, frac, has_second, level)
+            old = acc[tile_at, :members, :]
+            acc[tile_at, :members, :] = jnp.where(lane_ids == lane_at, value, old)
+
+        if raw:
+            for level in range(lev_rows):
+                pl.when(row == level)(functools.partial(put, level))
+        else:
+            put(0)
         return carry
 
     lax.fori_loop(0, count, body, 0)

time: 103 us -> 101 us (0.981)
  Pallas kernels: 102 us -> 100 us
where the time goes in v4:
time: 101 us
  Pallas kernels  100 us (99%)
    pallas_call x2, Pallas kernels, exchange(): pl.pallas_call(functools.partial(exchange_kernel, n_slab, n_lev, pieces),...  65 us
    pallas_call x2, Pallas kernels, pick(): pl.pallas_call(functools.partial(pick_kernel, block, members, lev_rows, n...  19.8 us
    pallas_call x2, Pallas kernels, update(): pl.pallas_call(functools.partial(update_kernel, block, lev_rows, raw_in,...  15.4 us

profile of v4, /device:TPU:0, one launch (start us, length us, event | category | flops | bytes accessed | tf_op | source)
XLA Modules:
  0.0 100.8 jit_solution(15538248033473496140)
XLA Ops:
  0.6 11.0 %pick.2 = f32[256,128]{1,0:T(8,128)} custom-call(s32[2,256]{1,0:T(2,128)} %cell_ref.3, f32[2,256]{1,0:T(2,128)} %frac_ref.3, f32[80,4,2304]{2,1,0:T(4,128)} %ens_ref.3), custom_call_target="tpu_custom_call" | custom-call | tf_op jit(solution)/shard_map/pick/pallas_call | solution.py:83
  11.7 33.7 %exchange.2 = (f32[32,8,128]{2,1,0:T(8,128)}, bf16[256,2304]{1,0:T(8,128)(2,1)}) custom-call(f32[32,8,128]{2,1,0:T(8,128)} %bitcast.7, bf16[2,64,2304]{2,1,0:T(8,128)(2,1)} %loc_ref.3), custom_call_target="tpu_custom_call" | custom-call | tf_op jit(solution)/shard_map/exchange/pallas_call | solution.py:205
  45.4 8.0 %update.2 = (f32[80,72,128]{2,1,0:T(8,128)}, f32[2,256]{1,0:T(2,128)}) custom-call(f32[256,128]{1,0:T(8,128)} %bitcast.10, f32[2,256]{1,0:T(2,128)} %value_ref.3, f32[2,256]{1,0:T(2,128)} %var_ref.3, f32[2,4,256]{2,1,0:T(4,128)} %bitcast.11, f32[2,256]{1,0:T(2,128)} %value_ref.3, bf16[256,2304]{1,0:T(8,128)(2,1)} %get-tuple-element.9.loc_ref, ...), custom_call_target="tpu_custom_call" | custom-call | tf_op jit(solution)/shard_map/update/pallas_call | solution.py:298
  53.4 8.8 %pick.3 = f32[256,128]{1,0:T(8,128)} custom-call(s32[2,256]{1,0:T(2,128)} %cell_ref.3, f32[2,256]{1,0:T(2,128)} %frac_ref.3, f32[5760,128]{1,0:T(8,128)} %bitcast.6), custom_call_target="tpu_custom_call" | custom-call | tf_op jit(solution)/shard_map/pick/pallas_call | solution.py:83
  62.2 31.2 %exchange.3 = (f32[32,8,128]{2,1,0:T(8,128)}, bf16[256,2304]{1,0:T(8,128)(2,1)}) custom-call(f32[32,8,128]{2,1,0:T(8,128)} %bitcast.8, bf16[2,64,2304]{2,1,0:T(8,128)(2,1)} %loc_ref.3), custom_call_target="tpu_custom_call" | custom-call | tf_op jit(solution)/shard_map/exchange/pallas_call | solution.py:205
  93.4 7.4 %update.3 = (f32[80,4,2304]{2,1,0:T(4,128)}, f32[2,256]{1,0:T(2,128)}) custom-call(f32[256,128]{1,0:T(8,128)} %bitcast.9, f32[2,256]{1,0:T(2,128)} %value_ref.3, f32[2,256]{1,0:T(2,128)} %var_ref.3, f32[2,4,256]{2,1,0:T(4,128)} %bitcast.12, f32[2,256]{1,0:T(2,128)} %get-tuple-element.12.old_ref, bf16[256,2304]{1,0:T(8,128)(2,1)} %get-tuple-element.13.loc_ref, ...), custom_call_target="tpu_custom_call" | custom-call | tf_op jit(solution)/shard_map/update/pallas_call | solution.py:298
